TPU v7x, 32 devices: a whole 2x2x4 slice. The times are simulated.
32 devices in a mesh: wide: 16 (over z, y, x), narrow: 2 (over core).
Axes of the slice: x: 2, y: 2, z: 4, core: 2. Of those that a mesh axis runs over, the one named last changes fastest.
Arguments:
- node_latent: bfloat16 [4096, 512], P(('wide', 'narrow')), may hold values from -6 to 6
- edge_latent: bfloat16 [16384, 512], P(('wide', 'narrow')), may hold values from -6 to 6
- node_cotangent: bfloat16 [4096, 512], P(('wide', 'narrow')), may hold values from -6 to 6
- w_first: bfloat16 [1536, 512], replicated, may hold values from -2 to 2
- bias_first: bfloat16 [512], replicated, may hold values from -4 to 4
- w_second: bfloat16 [512, 512], replicated, may hold values from -2 to 2
- bias_second: bfloat16 [512], replicated, may hold values from -4 to 4
- norm_gain: bfloat16 [512], replicated, may hold values from 0.099609375 to 1.8984375
- send_map: int32 [32, 4, 64], P(('wide', 'narrow')), may hold values from -1 to 127, as said below
- edge_sender: int32 [16384], P(('wide', 'narrow')), may hold values from 0 to 383, as said below
- edge_receiver: int32 [16384], P(('wide', 'narrow')), may hold values from 0 to 127
Outputs:
- node_grad: bfloat16 [4096, 512], P(('wide', 'narrow'))
- edge_grad: bfloat16 [16384, 512], P(('wide', 'narrow'))
- first_update: float32 [1536, 512], P('wide')
- second_update: float32 [512, 512], P('wide')
Inputs may be any that keep to these rules, and one draw needn't show every extreme that they name: `send_map`: -1 marks an unused slot; in each row the used slots come first, at most 64, about a third of them on average; in every draw some partition uses all 64 slots toward a wide neighbour; partitions at narrow index 0 send nothing toward block 3 of a lower neighbour and those at the last narrow index nothing toward a higher one. `edge_sender`: a value below 128 is a local node; 128 + k * 64 + s names slot s of received block k, and only slots that the sending partition uses are named.
All inputs are finite; a program needn't handle non-finite values.
Results may differ from a plain program's by a relative error of at most 0.0085.
Values may be sent and summed in bfloat16 or wider, within the bound.
No kernel may reach another device: no remote copies, remote signals or barrier semaphores. Data moves between devices by JAX's collectives and lax.ppermute only.
A program may use at most 64 MiB of HBM per device.

v0:
```python
import math
import jax
import jax.numpy as jnp
from jax import lax
from jax.sharding import PartitionSpec as P


def shifted(value, axis, steps):
    count = lax.axis_size(axis)
    pairs = [(source, (source + steps) % count) for source in range(count)]
    return lax.ppermute(value, axis, pairs)


def shifted_2(block, axis, distance):
    devices = range(lax.axis_size(axis))
    route = [(i - distance, i) for i in devices if i - distance in devices]
    return lax.ppermute(block, axis, route)


def neighbours(blocks, direction):
    higher = shifted(blocks[0], "wide", direction)
    lower = shifted(blocks[1], "wide", -direction)
    up_side = shifted_2(blocks[2], "narrow", direction)
    down_side = shifted_2(blocks[3], "narrow", -direction)
    return jnp.stack([higher, lower, up_side, down_side], 0)


def norm_parts(second_pre):
    mean_value = jnp.mean(second_pre, -1, keepdims=True)
    centered = second_pre - mean_value
    variance = jnp.mean(centered * centered, -1, keepdims=True)
    inv_std = lax.rsqrt(variance + 1e-05)
    return (centered * inv_std, inv_std)


def clip_share(grad_share, grad_sq, weight_sq, fan_rows):
    unit_ratio = jnp.sqrt((grad_sq + 1e-06) / (weight_sq + 1e-06))
    mean_ratio = jnp.mean(unit_ratio)
    factor = jnp.minimum(
        1.0 / (mean_ratio * jnp.sqrt(weight_sq + 1e-06)), 1.0 / jnp.sqrt(grad_sq + 1e-06)
    )
    return grad_share * factor * math.sqrt(fan_rows)


def edge_contract(hot_table, values):
    return lax.dot_general(
        hot_table,
        values,
        (((0,), (0,)), ((), ())),
        precision=lax.Precision.HIGHEST,
        preferred_element_type=jnp.float32,
    )


def per_device(
    node_latent,
    edge_latent,
    node_cotangent,
    w_first,
    bias_first,
    w_second,
    bias_second,
    norm_gain,
    send_map,
    edge_sender,
    edge_receiver,
):
    node_count, feature_width = node_latent.shape
    halo_slots = send_map.shape[2]
    table_rows = node_count + 4 * halo_slots
    send_hot = (send_map[0][:, :, None] == jnp.arange(node_count, dtype=jnp.int32)).astype(
        jnp.bfloat16
    )
    outgoing = jnp.einsum(
        "khn,nd->khd", send_hot, node_latent, preferred_element_type=jnp.float32
    ).astype(jnp.bfloat16)
    received = neighbours(outgoing, 1)
    node_table = jnp.concatenate([node_latent, received.reshape(4 * halo_slots, feature_width)], 0)
    sender_hot = (edge_sender[:, None] == jnp.arange(table_rows, dtype=jnp.int32)).astype(
        jnp.bfloat16
    )
    receiver_hot = (edge_receiver[:, None] == jnp.arange(node_count, dtype=jnp.int32)).astype(
        jnp.bfloat16
    )
    sender_rows = jnp.dot(sender_hot, node_table, preferred_element_type=jnp.float32).astype(
        jnp.bfloat16
    )
    receiver_rows = jnp.dot(receiver_hot, node_latent, preferred_element_type=jnp.float32).astype(
        jnp.bfloat16
    )
    inputs = jnp.concatenate([edge_latent, sender_rows, receiver_rows], 1)
    preact = jnp.dot(inputs, w_first, preferred_element_type=jnp.float32) + bias_first.astype(
        jnp.float32
    )
    activation = jax.nn.silu(preact).astype(jnp.bfloat16)
    second_pre = jnp.dot(
        activation, w_second, preferred_element_type=jnp.float32
    ) + bias_second.astype(jnp.float32)
    normalized, inv_std = norm_parts(second_pre)
    upstream = jnp.dot(receiver_hot, node_cotangent, preferred_element_type=jnp.float32)
    scaled = upstream * norm_gain.astype(jnp.float32)
    norm_back = (
        inv_std
        * (
            scaled
            - jnp.mean(scaled, -1, keepdims=True)
            - normalized * jnp.mean(scaled * normalized, -1, keepdims=True)
        )
    ).astype(jnp.bfloat16)
    second_grad = lax.dot_general(
        activation, norm_back, (((0,), (0,)), ((), ())), preferred_element_type=jnp.float32
    )
    sigmoid_pre = jax.nn.sigmoid(preact)
    pre_back = (
        jnp.dot(norm_back, w_second.T, preferred_element_type=jnp.float32)
        * sigmoid_pre
        * (1.0 + preact * (1.0 - sigmoid_pre))
    ).astype(jnp.bfloat16)
    first_grad = lax.dot_general(
        inputs, pre_back, (((0,), (0,)), ((), ())), preferred_element_type=jnp.float32
    )
    input_back = jnp.dot(pre_back, w_first.T, preferred_element_type=jnp.float32)
    edge_grad = (upstream + input_back[:, :feature_width]).astype(jnp.bfloat16)
    table_grad = edge_contract(
        sender_hot.astype(jnp.float32), input_back[:, feature_width : 2 * feature_width]
    )
    receiver_grad = edge_contract(
        receiver_hot.astype(jnp.float32), input_back[:, 2 * feature_width :]
    )
    halo_grad = table_grad[node_count:].reshape(4, halo_slots, feature_width).astype(jnp.bfloat16)
    returned = neighbours(halo_grad, -1)
    back = jnp.einsum("khn,khd->nd", send_hot, returned, preferred_element_type=jnp.float32)
    node_grad = (
        node_cotangent.astype(jnp.float32) + table_grad[:node_count] + receiver_grad + back
    ).astype(jnp.bfloat16)
    wide_count = lax.axis_size("wide")
    first_rows = w_first.shape[0] // wide_count
    second_rows = w_second.shape[0] // wide_count
    first_weight_sq = jnp.sum(jnp.square(w_first.astype(jnp.float32)), 0)
    second_weight_sq = jnp.sum(jnp.square(w_second.astype(jnp.float32)), 0)
    first_total, second_total = lax.psum((first_grad, second_grad), ("wide", "narrow"))
    position = lax.axis_index("wide")
    first_share = lax.dynamic_slice_in_dim(first_total, position * first_rows, first_rows, 0)
    second_share = lax.dynamic_slice_in_dim(second_total, position * second_rows, second_rows, 0)
    first_grad_sq = jnp.sum(first_total * first_total, 0)
    second_grad_sq = jnp.sum(second_total * second_total, 0)
    first_update = clip_share(first_share, first_grad_sq, first_weight_sq, w_first.shape[0])
    second_update = clip_share(second_share, second_grad_sq, second_weight_sq, w_second.shape[0])
    return (node_grad, edge_grad, first_update, second_update)


def solution(mesh):
    return jax.shard_map(
        per_device,
        mesh=mesh,
        in_specs=(
            P(("wide", "narrow"), None),
            P(("wide", "narrow"), None),
            P(("wide", "narrow"), None),
            P(),
            P(),
            P(),
            P(),
            P(),
            P(("wide", "narrow"), None, None),
            P(("wide", "narrow")),
            P(("wide", "narrow")),
        ),
        out_specs=(
            P(("wide", "narrow"), None),
            P(("wide", "narrow"), None),
            P("wide", None),
            P("wide", None),
        ),
        check_vma=False,
    )
```

profile of v0, /device:TPU:0, one launch (start us, length us, event | category | flops | bytes accessed | tf_op | source)
XLA Modules:
  0.0 192.4 jit_solution(14532633733271048976)
XLA Ops:
  7.2 0.0 copy-start.4
  7.2 0.0 copy-start.1
  7.2 0.0 all-reduce.3.cloned.1.call-start
  7.2 1.3 convolution_convert_fusion.2
  8.6 1.3 collective-permute-start.3
  9.9 3.0 %collective-permute-start.2 = (bf16[64,512]{1,0:T(8,128)(2,1)S(1)}, bf16[64,512]{1,0:T(8,128)(2,1)S(1)}, u32[]{:S(2)}, u32[]{:S(2)}) collective-permute-start(bf16[64,512]{1,0:T(8,128)(2,1)S(1)} %get-tuple-element.18), channel_id=1, source_target_pairs={{0,1},{2,3},{4,5},{6,7},{8,9},{10,11},{12,13},{14,15},{16,17},{18,... | collective-permute-start | bytes 196616 | tf_op jit(solution)/shard_map/ppermute | solution.py:17
  12.9 7.0 %collective-permute-start.1 = (bf16[64,512]{1,0:T(8,128)(2,1)S(1)}, bf16[64,512]{1,0:T(8,128)(2,1)S(1)}, u32[]{:S(2)}, u32[]{:S(2)}) collective-permute-start(bf16[64,512]{1,0:T(8,128)(2,1)S(1)} %get-tuple-element.19), channel_id=1, source_target_pairs={{0,30},{2,0},{4,2},{6,4},{8,6},{10,8},{12,10},{14,12},{16,14},{18,... | collective-permute-start | bytes 196616 | tf_op jit(solution)/shard_map/ppermute | solution.py:11
  19.9 1.3 convolution_convert_fusion.1
  21.3 0.7 convert_element_type.56
  22.0 0.7 convert_element_type.55
  22.6 1.3 copy.15
  23.9 0.7 convert_element_type.53
  24.6 3.2 %collective-permute-done = bf16[64,512]{1,0:T(8,128)(2,1)S(1)} collective-permute-done((bf16[64,512]{1,0:T(8,128)(2,1)S(1)}, bf16[64,512]{1,0:T(8,128)(2,1)S(1)}, u32[]{:S(2)}, u32[]{:S(2)}) %collective-permute-start) | collective-permute-done | bytes 65568 | tf_op jit(solution)/shard_map/ppermute | solution.py:11
  27.9 0.6 convolution_convert_fusion
  28.5 0.0 copy-start.5
  28.5 1.0 convolution_add_fusion.1
  29.5 0.0 copy-done.5
  29.5 0.6 fusion.33
  30.2 0.2 multiply_reduce_fusion.5
  30.4 0.1 copy-done.6
  30.4 0.5 multiply_reduce_fusion.6
  31.0 0.3 multiply_convert_fusion
  31.3 0.7 fusion.1
  31.9 0.1 copy-done
  32.0 1.5 fusion.31
  33.5 2.7 %fusion.7 = f32[1536,512]{1,0:T(8,128)} fusion(bf16[512,512]{1,0:T(8,128)(2,1)S(1)} %fusion.1, bf16[512,512]{0,1:T(8,128)(2,1)S(1)} %convolution_convert_fusion.1, bf16[512,512]{0,1:T(8,128)(2,1)S(1)} %convolution_convert_fusion, bf16[512,512]{0,1:T(8,128)(2,1)S(1)} %copy.15), kind=kOutput, calls=%fused_computation.28 | convolution fusion | flops 810024960 | bytes 5242880 | tf_op jit(solution)/shard_map/dot_general | solution.py:119
  36.2 0.0 all-reduce.3.cloned.1.call-update
  36.2 0.2 multiply_reduce_fusion.2
  36.4 0.4 multiply_reduce_fusion
  36.8 2.6 %fusion.35 = f32[512,1536]{1,0:T(8,128)S(1)} fusion(bf16[512,512]{1,0:T(8,128)(2,1)} %copy-done.3, bf16[1536,512]{1,0:T(8,128)(2,1)} %param.14), kind=kOutput, calls=%fused_computation.74 | convolution fusion | flops 805306368 | bytes 5242880 | tf_op jit(solution)/shard_map/dot_general | solution.py:122
  39.3 1.0 slice.69
  40.4 1.8 fusion.34
  42.3 1.9 collective-permute-start.7
  44.2 1.3 collective-permute-start.6
  45.5 0.1 collective-permute-start.5
  45.5 5.6 %collective-permute-start.4 = (bf16[64,512]{1,0:T(8,128)(2,1)S(1)}, bf16[64,512]{1,0:T(8,128)(2,1)}, u32[]{:S(2)}, u32[]{:S(2)}) collective-permute-start(bf16[64,512]{1,0:T(8,128)(2,1)S(1)} %get-tuple-element.12), channel_id=1, source_target_pairs={{0,30},{2,0},{4,2},{6,4},{8,6},{10,8},{12,10},{14,12},{16,14},{18,... | collective-permute-start | bytes 196616 | tf_op jit(solution)/shard_map/ppermute | solution.py:11
  51.1 2.6 %copy.18 = f32[512,512]{0,1:T(8,128)} copy(f32[512,512]{1,0:T(8,128)} %slice.69) | data formatting | bytes 2097152
  53.7 2.6 %add_convert_fusion = bf16[512,512]{0,1:T(8,128)(2,1)} fusion(f32[512,512]{0,1:T(8,128)} %copy-done, f32[512,512]{0,1:T(8,128)} %copy.18), kind=kLoop, calls=%fused_computation.20 | loop fusion | flops 524288 | bytes 2621440 | tf_op jit(solution)/shard_map/convert_element_type | solution.py:123
  56.2 2.3 %convolution_add_fusion.2 = f32[128,512]{1,0:T(8,128)} fusion(f32[512,1536]{1,0:T(8,128)S(1)} %fusion.35, f32[384,512]{1,0:T(8,128)} %get-tuple-element.24, bf16[128,512]{1,0:T(8,128)(2,1)S(1)} %copy-done.6, s32[512]{0:T(512)S(1)} %copy-done.7), kind=kOutput, calls=%fused_computation.12 | convolution fusion | flops 402915328 | bytes 1705984 | tf_op jit(solution)/shard_map/dot_general | solution.py:46
  58.5 2.0 %copy.17 = bf16[512,512]{1,0:T(8,128)(2,1)} copy(bf16[512,512]{0,1:T(8,128)(2,1)} %add_convert_fusion) | data formatting | bytes 1048576
  60.6 2.0 %fusion.3 = bf16[128,512]{1,0:T(8,128)(2,1)} fusion(f32[128,512]{1,0:T(8,128)} %convolution_add_fusion.2, bf16[1,64,512]{2,1,0:T(8,128)(2,1)} %bitcast.14, bf16[1,64,512]{2,1,0:T(8,128)(2,1)} %bitcast.13, bf16[1,64,512]{2,1,0:T(8,128)(2,1)} %bitcast.12, bf16[1,64,512]{2,1,0:T(8,128)(2,1)} %bitcast.11, s32[4,64]{1,0:T(4,128)S(1)} %bitcast.43), kind=kOutput, calls=%fused_computation.14 | convolution fusion | flops 34111488 | bytes 656384 | tf_op jit(solution)/shard_map/khn,khd->nd/dot_general | solution.py:132
  62.6 115.6 %all-reduce.3.cloned.1.call-done = (f32[1536,512]{1,0:T(8,128)}, f32[512,512]{1,0:T(8,128)}) async-done(((f32[1536,512]{1,0:T(8,128)}, f32[512,512]{1,0:T(8,128)}), (f32[1536,512]{1,0:T(8,128)}, f32[512,512]{1,0:T(8,128)})) %all-reduce.3.cloned.1.call-update) | async-done | bytes 4194320 | tf_op jit(solution)/shard_map/psum | solution.py:141
  178.3 2.3 %multiply_reduce_fusion.1 = f32[512]{0:T(512)S(1)} fusion(f32[1536,512]{1,0:T(8,128)} %get-tuple-element.10), kind=kLoop, calls=%fused_computation.1 | loop fusion | flops 1572352 | bytes 3147776 | tf_op jit(solution)/shard_map/reduce_sum | solution.py:145
  180.5 0.6 sqrt_reduce_fusion.1
  181.8 0.1 multiply_reduce_fusion.3
  182.0 0.6 sqrt_reduce_fusion
  183.2 1.6 multiply_multiply_fusion
  184.9 0.6 multiply_multiply_fusion.1
  (30 shorter events, 0.2 us)
Async XLA Ops:
  7.2 20.7 %copy-start.4 = (bf16[128,512]{1,0:T(8,128)(2,1)S(1)}, bf16[128,512]{1,0:T(8,128)(2,1)}, u32[]{:S(2)}) copy-start(bf16[128,512]{1,0:T(8,128)(2,1)} %param.11) | copy-start | bytes 393220
  7.2 20.7 %copy-start.8 = (s32[512]{0:T(512)S(1)}, s32[512]{0:T(512)}, u32[]{:S(2)}) copy-start(s32[512]{0:T(512)} %param.20) | copy-start | bytes 6148
  7.2 21.3 %copy-start.1 = (bf16[1536,512]{1,0:T(8,128)(2,1)S(1)}, bf16[1536,512]{1,0:T(8,128)(2,1)}, u32[]{:S(2)}) copy-start(bf16[1536,512]{1,0:T(8,128)(2,1)} %param.14) | copy-start | bytes 4718596
  7.2 171.1 %all-reduce.3.cloned.1.call-start = ((), (), s32[]{:S(2)}) async-start(), calls=%async_computation | async-start | bytes 8388608 | tf_op jit(solution)/shard_map/psum | solution.py:141
  8.6 16.0 %collective-permute-start.3 = (bf16[64,512]{1,0:T(8,128)(2,1)S(1)}, bf16[64,512]{1,0:T(8,128)(2,1)S(1)}, u32[]{:S(2)}, u32[]{:S(2)}) collective-permute-start(bf16[64,512]{1,0:T(8,128)(2,1)S(1)} %get-tuple-element.17), channel_id=1, source_target_pairs={{1,0},{3,2},{5,4},{7,6},{9,8},{11,10},{13,12},{15,14},{17,16},{19,... | collective-permute-start | bytes 196616 | tf_op jit(solution)/shard_map/ppermute | solution.py:17
  9.9 14.7 %collective-permute-start.2 = (bf16[64,512]{1,0:T(8,128)(2,1)S(1)}, bf16[64,512]{1,0:T(8,128)(2,1)S(1)}, u32[]{:S(2)}, u32[]{:S(2)}) collective-permute-start(bf16[64,512]{1,0:T(8,128)(2,1)S(1)} %get-tuple-element.18), channel_id=1, source_target_pairs={{0,1},{2,3},{4,5},{6,7},{8,9},{10,11},{12,13},{14,15},{16,17},{18,... | collective-permute-start | bytes 196616 | tf_op jit(solution)/shard_map/ppermute | solution.py:17
  12.9 11.7 %collective-permute-start.1 = (bf16[64,512]{1,0:T(8,128)(2,1)S(1)}, bf16[64,512]{1,0:T(8,128)(2,1)S(1)}, u32[]{:S(2)}, u32[]{:S(2)}) collective-permute-start(bf16[64,512]{1,0:T(8,128)(2,1)S(1)} %get-tuple-element.19), channel_id=1, source_target_pairs={{0,30},{2,0},{4,2},{6,4},{8,6},{10,8},{12,10},{14,12},{16,14},{18,... | collective-permute-start | bytes 196616 | tf_op jit(solution)/shard_map/ppermute | solution.py:11
  19.9 7.9 %collective-permute-start = (bf16[64,512]{1,0:T(8,128)(2,1)S(1)}, bf16[64,512]{1,0:T(8,128)(2,1)S(1)}, u32[]{:S(2)}, u32[]{:S(2)}) collective-permute-start(bf16[64,512]{1,0:T(8,128)(2,1)S(1)} %get-tuple-element.16), channel_id=1, source_target_pairs={{0,2},{2,4},{4,6},{6,8},{8,10},{10,12},{12,14},{14,16},{16,18},{18... | collective-permute-start | bytes 196616 | tf_op jit(solution)/shard_map/ppermute | solution.py:11
  28.5 1.0 copy-start.5
  29.5 0.9 copy-start.6
  29.5 0.9 copy-start.7
  30.9 1.1 copy-start
  32.0 1.5 copy-start.3
  42.3 18.3 %collective-permute-start.7 = (bf16[64,512]{1,0:T(8,128)(2,1)S(1)}, bf16[64,512]{1,0:T(8,128)(2,1)}, u32[]{:S(2)}, u32[]{:S(2)}) collective-permute-start(bf16[64,512]{1,0:T(8,128)(2,1)S(1)} %get-tuple-element.13), channel_id=1, source_target_pairs={{0,1},{2,3},{4,5},{6,7},{8,9},{10,11},{12,13},{14,15},{16,17},{18,... | collective-permute-start | bytes 196616 | tf_op jit(solution)/shard_map/ppermute | solution.py:17
  44.2 16.4 %collective-permute-start.6 = (bf16[64,512]{1,0:T(8,128)(2,1)S(1)}, bf16[64,512]{1,0:T(8,128)(2,1)}, u32[]{:S(2)}, u32[]{:S(2)}) collective-permute-start(bf16[64,512]{1,0:T(8,128)(2,1)S(1)} %get-tuple-element.14), channel_id=1, source_target_pairs={{1,0},{3,2},{5,4},{7,6},{9,8},{11,10},{13,12},{15,14},{17,16},{19,... | collective-permute-start | bytes 196616 | tf_op jit(solution)/shard_map/ppermute | solution.py:17
  45.5 15.1 %collective-permute-start.5 = (bf16[64,512]{1,0:T(8,128)(2,1)S(1)}, bf16[64,512]{1,0:T(8,128)(2,1)}, u32[]{:S(2)}, u32[]{:S(2)}) collective-permute-start(bf16[64,512]{1,0:T(8,128)(2,1)S(1)} %get-tuple-element.15), channel_id=1, source_target_pairs={{0,2},{2,4},{4,6},{6,8},{8,10},{10,12},{12,14},{14,16},{16,18},{18... | collective-permute-start | bytes 196616 | tf_op jit(solution)/shard_map/ppermute | solution.py:11
  45.5 15.0 %collective-permute-start.4 = (bf16[64,512]{1,0:T(8,128)(2,1)S(1)}, bf16[64,512]{1,0:T(8,128)(2,1)}, u32[]{:S(2)}, u32[]{:S(2)}) collective-permute-start(bf16[64,512]{1,0:T(8,128)(2,1)S(1)} %get-tuple-element.12), channel_id=1, source_target_pairs={{0,30},{2,0},{4,2},{6,4},{8,6},{10,8},{12,10},{14,12},{16,14},{18,... | collective-permute-start | bytes 196616 | tf_op jit(solution)/shard_map/ppermute | solution.py:11
  53.7 6.9 %copy-start.9 = (s32[1,4,64]{2,1,0:T(4,128)S(1)}, s32[1,4,64]{2,1,0:T(4,128)}, u32[]{:S(2)}) copy-start(s32[1,4,64]{2,1,0:T(4,128)} %param.19) | copy-start | bytes 3076
  178.3 3.5 %copy-start.2 = (f32[512,512]{1,0:T(8,128)S(1)}, f32[512,512]{1,0:T(8,128)}, u32[]{:S(2)}) copy-start(f32[512,512]{1,0:T(8,128)} %get-tuple-element.11) | copy-start | bytes 3145732
Sparse Core Ops, SparseCore 0:
  36.3 141.9 all-reduce.2
where the time goes:
time: 193 us; the launch traced here: 192 us
  waiting for transfers between devices  119 us (62%)
  starting transfers between devices  20.2 us (10%)
  matrix products  18.9 us (10%)
  between operations  15.6 us (8%)
  other arithmetic  11.6 us (6%)
  local copies, waits for them, and re-layouts  7.15 us (4%)
    psum x1, waiting for transfers between devices, per_device(): lax.psum((first_grad, second_grad), ('wide', 'narrow'))  116 us
    ppermute x4, starting transfers between devices, shifted(): return lax.ppermute(value, axis, pairs)  12.7 us
    ppermute x4, starting transfers between devices, shifted_2(): return lax.ppermute(block, axis, route)  7.52 us
    unnamed x23, local copies, waits for them, and re-layouts  6.07 us
    dot_general x2, matrix products, edge_contract(): lax.dot_general(hot_table, values, (((0,), (0,)), ((), ())), precision=la...  4.11 us
  transfers between devices with their start and end apart: 9, of which 2 were waited for; matrix products, arithmetic and copies ran while one was open for 12% of the time, Pallas kernels for 0%

commit v1 on v0

--- a/solution.py
+++ b/solution.py
@@ -138,7 +138,7 @@
     second_rows = w_second.shape[0] // wide_count
     first_weight_sq = jnp.sum(jnp.square(w_first.astype(jnp.float32)), 0)
     second_weight_sq = jnp.sum(jnp.square(w_second.astype(jnp.float32)), 0)
-    first_total, second_total = lax.psum((first_grad, second_grad), ("wide", "narrow"))
+    first_total, second_total = lax.psum(lax.psum((first_grad, second_grad), "narrow"), "wide")
     position = lax.axis_index("wide")
     first_share = lax.dynamic_slice_in_dim(first_total, position * first_rows, first_rows, 0)
     second_share = lax.dynamic_slice_in_dim(second_total, position * second_rows, second_rows, 0)

time: 193 us -> 254 us (1.32)
  waiting for transfers between devices: 119 us -> 179 us
    psum x1 -> x2, waiting for transfers between devices: 116 us -> 176 us  [the longest x1 149 us: per_device(): lax.psum(lax.psum((first_grad, second_grad), 'narrow'), 'wide')]
  transfers between devices with their start and end apart: 9 -> 10, of which waited for: 2 -> 3; matrix products, arithmetic and copies ran while one was open for 12% -> 9% of each run, Pallas kernels for 0% -> 0%
where the time goes in v1:
time: 254 us
  waiting for transfers between devices  179 us (70%)
  starting transfers between devices  21.1 us (8%)
  matrix products  18.9 us (7%)
  between operations  15.6 us (6%)
  other arithmetic  11.5 us (5%)
  local copies, waits for them, and re-layouts  7.14 us (3%)
    psum x1, waiting for transfers between devices, per_device(): lax.psum(lax.psum((first_grad, second_grad), 'narrow'), 'wide')  149 us
    psum x1, waiting for transfers between devices, per_device(): lax.psum((first_grad, second_grad), 'narrow')  26.6 us
    ppermute x4, starting transfers between devices, shifted(): return lax.ppermute(value, axis, pairs)  12.7 us
    ppermute x4, starting transfers between devices, shifted_2(): return lax.ppermute(block, axis, route)  8.36 us
    unnamed x23, local copies, waits for them, and re-layouts  6.06 us
  transfers between devices with their start and end apart: 10, of which 3 were waited for; matrix products, arithmetic and copies ran while one was open for 9% of the time, Pallas kernels for 0%

profile of v1, /device:TPU:0, one launch (start us, length us, event | category | flops | bytes accessed | tf_op | source)
XLA Modules:
  0.0 253.6 jit_solution(11567867524157199663)
XLA Ops:
  7.2 0.0 all-reduce.7.cloned.1.call-start
  7.2 1.3 convolution_convert_fusion.2
  8.6 1.3 collective-permute-start.3
  9.9 3.0 %collective-permute-start.2 = (bf16[64,512]{1,0:T(8,128)(2,1)S(1)}, bf16[64,512]{1,0:T(8,128)(2,1)S(1)}, u32[]{:S(2)}, u32[]{:S(2)}) collective-permute-start(bf16[64,512]{1,0:T(8,128)(2,1)S(1)} %get-tuple-element.20), channel_id=1, source_target_pairs={{0,1},{2,3},{4,5},{6,7},{8,9},{10,11},{12,13},{14,15},{16,17},{18,... | collective-permute-start | bytes 196616 | tf_op jit(solution)/shard_map/ppermute | solution.py:17
  12.9 7.0 %collective-permute-start.1 = (bf16[64,512]{1,0:T(8,128)(2,1)S(1)}, bf16[64,512]{1,0:T(8,128)(2,1)S(1)}, u32[]{:S(2)}, u32[]{:S(2)}) collective-permute-start(bf16[64,512]{1,0:T(8,128)(2,1)S(1)} %get-tuple-element.21), channel_id=1, source_target_pairs={{0,30},{2,0},{4,2},{6,4},{8,6},{10,8},{12,10},{14,12},{16,14},{18,... | collective-permute-start | bytes 196616 | tf_op jit(solution)/shard_map/ppermute | solution.py:11
  19.9 1.3 convolution_convert_fusion.1
  21.3 0.7 convert_element_type.56
  22.0 0.7 convert_element_type.55
  22.6 1.3 copy.15
  23.9 0.7 convert_element_type.53
  24.6 3.2 %collective-permute-done = bf16[64,512]{1,0:T(8,128)(2,1)S(1)} collective-permute-done((bf16[64,512]{1,0:T(8,128)(2,1)S(1)}, bf16[64,512]{1,0:T(8,128)(2,1)S(1)}, u32[]{:S(2)}, u32[]{:S(2)}) %collective-permute-start) | collective-permute-done | bytes 65568 | tf_op jit(solution)/shard_map/ppermute | solution.py:11
  27.9 0.6 convolution_convert_fusion
  28.5 1.0 convolution_add_fusion.1
  29.5 0.0 copy-done.5
  29.5 0.6 fusion.33
  30.2 0.2 multiply_reduce_fusion.5
  30.4 0.1 copy-done.6
  30.4 0.5 multiply_reduce_fusion.6
  31.0 0.3 multiply_convert_fusion
  31.3 0.7 fusion.1
  31.9 0.1 copy-done
  32.0 1.5 fusion.31
  33.5 2.7 %fusion.7 = f32[1536,512]{1,0:T(8,128)} fusion(bf16[512,512]{1,0:T(8,128)(2,1)S(1)} %fusion.1, bf16[512,512]{0,1:T(8,128)(2,1)S(1)} %convolution_convert_fusion.1, bf16[512,512]{0,1:T(8,128)(2,1)S(1)} %convolution_convert_fusion, bf16[512,512]{0,1:T(8,128)(2,1)S(1)} %copy.15), kind=kOutput, calls=%fused_computation.28 | convolution fusion | flops 810024960 | bytes 5242880 | tf_op jit(solution)/shard_map/dot_general | solution.py:119
  36.2 0.0 all-reduce.7.cloned.1.call-update
  36.2 0.0 all-reduce.5.cloned.1.call-start
  36.2 26.6 %all-reduce.7.cloned.1.call-done = (f32[1536,512]{1,0:T(8,128)}, f32[512,512]{1,0:T(8,128)}) async-done(((f32[1536,512]{1,0:T(8,128)}, f32[512,512]{1,0:T(8,128)}), (f32[1536,512]{1,0:T(8,128)}, f32[512,512]{1,0:T(8,128)})) %all-reduce.7.cloned.1.call-update) | async-done | bytes 4194320 | tf_op jit(solution)/shard_map/psum | solution.py:141
  62.9 0.0 all-reduce.5.cloned.1.call-update
  62.9 0.2 multiply_reduce_fusion.2
  63.1 0.4 multiply_reduce_fusion
  63.5 2.6 %fusion.35 = f32[512,1536]{1,0:T(8,128)S(1)} fusion(bf16[512,512]{1,0:T(8,128)(2,1)} %copy-done.3, bf16[1536,512]{1,0:T(8,128)(2,1)} %param.14), kind=kOutput, calls=%fused_computation.74 | convolution fusion | flops 805306368 | bytes 5242880 | tf_op jit(solution)/shard_map/dot_general | solution.py:122
  66.1 1.0 slice.69
  67.1 1.9 fusion.34
  69.0 2.8 %collective-permute-start.7 = (bf16[64,512]{1,0:T(8,128)(2,1)S(1)}, bf16[64,512]{1,0:T(8,128)(2,1)}, u32[]{:S(2)}, u32[]{:S(2)}) collective-permute-start(bf16[64,512]{1,0:T(8,128)(2,1)S(1)} %get-tuple-element.15), channel_id=1, source_target_pairs={{0,1},{2,3},{4,5},{6,7},{8,9},{10,11},{12,13},{14,15},{16,17},{18,... | collective-permute-start | bytes 196616 | tf_op jit(solution)/shard_map/ppermute | solution.py:17
  71.7 1.3 collective-permute-start.6
  73.0 1.9 collective-permute-start.5
  74.9 3.8 %collective-permute-start.4 = (bf16[64,512]{1,0:T(8,128)(2,1)S(1)}, bf16[64,512]{1,0:T(8,128)(2,1)}, u32[]{:S(2)}, u32[]{:S(2)}) collective-permute-start(bf16[64,512]{1,0:T(8,128)(2,1)S(1)} %get-tuple-element.14), channel_id=1, source_target_pairs={{0,30},{2,0},{4,2},{6,4},{8,6},{10,8},{12,10},{14,12},{16,14},{18,... | collective-permute-start | bytes 196616 | tf_op jit(solution)/shard_map/ppermute | solution.py:11
  78.7 2.5 %copy.18 = f32[512,512]{0,1:T(8,128)} copy(f32[512,512]{1,0:T(8,128)} %slice.69) | data formatting | bytes 2097152
  81.2 2.5 add_convert_fusion
  83.7 2.3 convolution_add_fusion.2
  86.0 2.0 copy.17
  88.1 2.0 fusion.3
  90.1 149.4 %all-reduce.5.cloned.1.call-done = (f32[1536,512]{1,0:T(8,128)}, f32[512,512]{1,0:T(8,128)}) async-done(((f32[1536,512]{1,0:T(8,128)}, f32[512,512]{1,0:T(8,128)}), (f32[1536,512]{1,0:T(8,128)}, f32[512,512]{1,0:T(8,128)})) %all-reduce.5.cloned.1.call-update) | async-done | bytes 4194320 | tf_op jit(solution)/shard_map/psum | solution.py:141
  239.5 2.3 multiply_reduce_fusion.1
  241.7 0.6 sqrt_reduce_fusion.1
  243.0 0.1 multiply_reduce_fusion.3
  243.2 0.6 sqrt_reduce_fusion
  244.4 1.6 multiply_multiply_fusion
  246.1 0.6 multiply_multiply_fusion.1
  (33 shorter events, 0.2 us)
Async XLA Ops:
  7.2 20.7 %copy-start.4 = (bf16[128,512]{1,0:T(8,128)(2,1)S(1)}, bf16[128,512]{1,0:T(8,128)(2,1)}, u32[]{:S(2)}) copy-start(bf16[128,512]{1,0:T(8,128)(2,1)} %param.11) | copy-start | bytes 393220
  7.2 20.7 %copy-start.8 = (s32[512]{0:T(512)S(1)}, s32[512]{0:T(512)}, u32[]{:S(2)}) copy-start(s32[512]{0:T(512)} %param.20) | copy-start | bytes 6148
  7.2 21.3 %copy-start.1 = (bf16[1536,512]{1,0:T(8,128)(2,1)S(1)}, bf16[1536,512]{1,0:T(8,128)(2,1)}, u32[]{:S(2)}) copy-start(bf16[1536,512]{1,0:T(8,128)(2,1)} %param.14) | copy-start | bytes 4718596
  7.2 55.7 %all-reduce.7.cloned.1.call-start = ((), (), s32[]{:S(2)}) async-start(), calls=%async_computation.1 | async-start | bytes 8388608 | tf_op jit(solution)/shard_map/psum | solution.py:141
  8.6 16.0 %collective-permute-start.3 = (bf16[64,512]{1,0:T(8,128)(2,1)S(1)}, bf16[64,512]{1,0:T(8,128)(2,1)S(1)}, u32[]{:S(2)}, u32[]{:S(2)}) collective-permute-start(bf16[64,512]{1,0:T(8,128)(2,1)S(1)} %get-tuple-element.19), channel_id=1, source_target_pairs={{1,0},{3,2},{5,4},{7,6},{9,8},{11,10},{13,12},{15,14},{17,16},{19,... | collective-permute-start | bytes 196616 | tf_op jit(solution)/shard_map/ppermute | solution.py:17
  9.9 14.7 %collective-permute-start.2 = (bf16[64,512]{1,0:T(8,128)(2,1)S(1)}, bf16[64,512]{1,0:T(8,128)(2,1)S(1)}, u32[]{:S(2)}, u32[]{:S(2)}) collective-permute-start(bf16[64,512]{1,0:T(8,128)(2,1)S(1)} %get-tuple-element.20), channel_id=1, source_target_pairs={{0,1},{2,3},{4,5},{6,7},{8,9},{10,11},{12,13},{14,15},{16,17},{18,... | collective-permute-start | bytes 196616 | tf_op jit(solution)/shard_map/ppermute | solution.py:17
  12.9 11.7 %collective-permute-start.1 = (bf16[64,512]{1,0:T(8,128)(2,1)S(1)}, bf16[64,512]{1,0:T(8,128)(2,1)S(1)}, u32[]{:S(2)}, u32[]{:S(2)}) collective-permute-start(bf16[64,512]{1,0:T(8,128)(2,1)S(1)} %get-tuple-element.21), channel_id=1, source_target_pairs={{0,30},{2,0},{4,2},{6,4},{8,6},{10,8},{12,10},{14,12},{16,14},{18,... | collective-permute-start | bytes 196616 | tf_op jit(solution)/shard_map/ppermute | solution.py:11
  19.9 7.9 %collective-permute-start = (bf16[64,512]{1,0:T(8,128)(2,1)S(1)}, bf16[64,512]{1,0:T(8,128)(2,1)S(1)}, u32[]{:S(2)}, u32[]{:S(2)}) collective-permute-start(bf16[64,512]{1,0:T(8,128)(2,1)S(1)} %get-tuple-element.18), channel_id=1, source_target_pairs={{0,2},{2,4},{4,6},{6,8},{8,10},{10,12},{12,14},{14,16},{16,18},{18... | collective-permute-start | bytes 196616 | tf_op jit(solution)/shard_map/ppermute | solution.py:11
  28.5 1.0 copy-start.5
  29.5 0.9 copy-start.6
  29.5 0.9 copy-start.7
  30.9 1.1 copy-start
  32.0 1.5 copy-start.3
  36.2 203.3 %all-reduce.5.cloned.1.call-start = ((), (), s32[]{:S(2)}) async-start(), calls=%async_computation | async-start | bytes 8388608 | tf_op jit(solution)/shard_map/psum | solution.py:141
  69.0 19.1 %collective-permute-start.7 = (bf16[64,512]{1,0:T(8,128)(2,1)S(1)}, bf16[64,512]{1,0:T(8,128)(2,1)}, u32[]{:S(2)}, u32[]{:S(2)}) collective-permute-start(bf16[64,512]{1,0:T(8,128)(2,1)S(1)} %get-tuple-element.15), channel_id=1, source_target_pairs={{0,1},{2,3},{4,5},{6,7},{8,9},{10,11},{12,13},{14,15},{16,17},{18,... | collective-permute-start | bytes 196616 | tf_op jit(solution)/shard_map/ppermute | solution.py:17
  71.7 16.3 %collective-permute-start.6 = (bf16[64,512]{1,0:T(8,128)(2,1)S(1)}, bf16[64,512]{1,0:T(8,128)(2,1)}, u32[]{:S(2)}, u32[]{:S(2)}) collective-permute-start(bf16[64,512]{1,0:T(8,128)(2,1)S(1)} %get-tuple-element.16), channel_id=1, source_target_pairs={{1,0},{3,2},{5,4},{7,6},{9,8},{11,10},{13,12},{15,14},{17,16},{19,... | collective-permute-start | bytes 196616 | tf_op jit(solution)/shard_map/ppermute | solution.py:17
  73.0 15.0 %collective-permute-start.5 = (bf16[64,512]{1,0:T(8,128)(2,1)S(1)}, bf16[64,512]{1,0:T(8,128)(2,1)}, u32[]{:S(2)}, u32[]{:S(2)}) collective-permute-start(bf16[64,512]{1,0:T(8,128)(2,1)S(1)} %get-tuple-element.17), channel_id=1, source_target_pairs={{0,2},{2,4},{4,6},{6,8},{8,10},{10,12},{12,14},{14,16},{16,18},{18... | collective-permute-start | bytes 196616 | tf_op jit(solution)/shard_map/ppermute | solution.py:11
  74.9 13.2 %collective-permute-start.4 = (bf16[64,512]{1,0:T(8,128)(2,1)S(1)}, bf16[64,512]{1,0:T(8,128)(2,1)}, u32[]{:S(2)}, u32[]{:S(2)}) collective-permute-start(bf16[64,512]{1,0:T(8,128)(2,1)S(1)} %get-tuple-element.14), channel_id=1, source_target_pairs={{0,30},{2,0},{4,2},{6,4},{8,6},{10,8},{12,10},{14,12},{16,14},{18,... | collective-permute-start | bytes 196616 | tf_op jit(solution)/shard_map/ppermute | solution.py:11
  81.2 6.8 %copy-start.9 = (s32[1,4,64]{2,1,0:T(4,128)S(1)}, s32[1,4,64]{2,1,0:T(4,128)}, u32[]{:S(2)}) copy-start(s32[1,4,64]{2,1,0:T(4,128)} %param.19) | copy-start | bytes 3076
  239.5 3.5 %copy-start.2 = (f32[512,512]{1,0:T(8,128)S(1)}, f32[512,512]{1,0:T(8,128)}, u32[]{:S(2)}) copy-start(f32[512,512]{1,0:T(8,128)} %get-tuple-element.11) | copy-start | bytes 3145732
Sparse Core Ops, SparseCore 0:
  36.3 26.5 all-reduce.6
  68.6 170.8 all-reduce.4
